TPU v7x, 32 devices: a whole 2x2x4 slice. The times are simulated.
32 devices in a mesh: patch: 8 (over z, y), sub: 4 (over x, core).
Axes of the slice: x: 2, y: 2, z: 4, core: 2. Of those that a mesh axis runs over, the one named last changes fastest.
Arguments:
- sources: int32 [128, 2], replicated, may hold values from 0 to 16383
- diag_coef: float32 [16384], P(('patch', 'sub')), may hold values from 1 to 2
- tiles: float32 [128, 6, 128, 128], P(('patch', 'sub')), may hold values from -0.109375 to 0.109375
- tile_cols: int32 [128, 6], P(('patch', 'sub')), may hold values from 0 to 7
- send_rows: int32 [32, 4, 128], P(('patch', 'sub')), may hold values from 0 to 511
- recv_rows: int32 [32, 512], P(('patch', 'sub')), may hold values from 0 to 511, each once within a row
- bounds: float32 [2], replicated, may hold values from 0.3 to 3.2, as said below
Outputs:
- solution: float32 [16384, 128], P(('patch', 'sub'))
- res_norm: float32 [128], replicated
Inputs may be any that keep to these rules, and one draw needn't show every extreme that they name: bounds[0] lies in 0.3 to 0.5 and bounds[1] in 2.6 to 3.2.
All inputs are finite; a program needn't handle non-finite values.
Results may differ from a plain program's by a relative error of at most 0.0001.
Values sent between devices are 32-bit elements; how exact they have to be, the bound alone decides.
A program may use at most 64 MiB of HBM per device.

v0:
```python
import jax
import jax.numpy as jnp
from jax import lax
from jax.sharding import PartitionSpec as P

ITERS = 8


def shifted(value, axis, steps):
    count = lax.axis_size(axis)
    pairs = [(source, (source + steps) % count) for source in range(count)]
    return lax.ppermute(value, axis, pairs)


def on_device(sources, diag_coef, tiles, tile_cols, send_rows, recv_rows, bounds):
    rows = diag_coef.shape[0]
    columns = sources.shape[0]
    blk_rows = tiles.shape[0]
    per_row = tiles.shape[1]
    tile_size = tiles.shape[2]
    sends = send_rows[0]
    receives = recv_rows[0]
    device = lax.axis_index("patch") * lax.axis_size("sub") + lax.axis_index("sub")
    local_ids = sources - device * rows
    inside = (local_ids >= 0) & (local_ids < rows)
    which = jnp.arange(columns, dtype=jnp.int32)[:, None]
    flat_index = jnp.where(inside, local_ids * columns + which, rows * columns).reshape(-1)
    counts = jax.ops.segment_sum(
        jnp.ones(flat_index.shape, jnp.float32), flat_index, num_segments=rows * columns + 1
    )
    right_side = counts[: rows * columns].reshape(rows, columns)

    def operate(field):
        packed = field[sends]
        below_patch = shifted(packed[1], "patch", 1)
        above_patch = shifted(packed[0], "patch", -1)
        below_sub = shifted(packed[3], "sub", 1)
        above_sub = shifted(packed[2], "sub", -1)
        received = jnp.concatenate([below_patch, above_patch, below_sub, above_sub], axis=0)
        halo_rows = received[receives]
        extended = jnp.concatenate([field, halo_rows], axis=0).reshape(-1, tile_size, columns)
        summed = jnp.zeros((blk_rows, tile_size, columns), jnp.float32)
        for slot_index in range(per_row):
            summed = summed + jnp.einsum(
                "bij,bjk->bik",
                tiles[:, slot_index],
                extended[tile_cols[:, slot_index]],
                precision=lax.Precision.HIGHEST,
            )
        return diag_coef[:, None] * field + summed.reshape(rows, columns)

    centre = (bounds[0] + bounds[1]) / 2.0
    half_width = (bounds[1] - bounds[0]) / 2.0
    ratio = centre / half_width
    damping = 1.0 / ratio
    solution = jnp.zeros_like(right_side)
    residual = right_side
    direction = right_side / centre
    for iteration in range(ITERS):
        solution = solution + direction
        residual = residual - operate(direction)
        if iteration + 1 < ITERS:
            damping_next = 1.0 / (2.0 * ratio - damping)
            direction = (
                damping_next * damping * direction + 2.0 * damping_next / half_width * residual
            )
            damping = damping_next
    final = right_side - operate(solution)
    squares = lax.psum(jnp.sum(final * final, axis=0), ("patch", "sub"))
    return (solution, jnp.sqrt(squares))


def solution(mesh):
    return jax.shard_map(
        on_device,
        mesh=mesh,
        in_specs=(
            P(),
            P(("patch", "sub")),
            P(("patch", "sub"), None, None, None),
            P(("patch", "sub"), None),
            P(("patch", "sub"), None, None),
            P(("patch", "sub"), None),
            P(),
        ),
        out_specs=(P(("patch", "sub"), None), P()),
        check_vma=False,
    )
```

profile of v0, /device:TPU:0, one launch (start us, length us, event | category | flops | bytes accessed | tf_op | source)
XLA Modules:
  0.0 229.8 jit_solution(4072987159246424181)
XLA Ops:
  4.9 2.3 %scatter_custom_fusion = f32[65537]{0:T(1024)S(1)} fusion(s32[256]{0:T(256)S(1)} %reshape.649, f32[256]{0:T(256)S(1)} %broadcast.65, f32[]{:T(128)} %constant.13.clone.1), kind=kCustom, calls=%fused_computation.254 | custom fusion | flops 256 | bytes 262152 | tf_op jit(solution)/shard_map/scatter-add | solution.py:28
  8.4 3.1 %collective-permute-start = (f32[128,128]{1,0:T(8,128)S(1)}, f32[128,128]{1,0:T(8,128)S(1)}, u32[]{:S(2)}, u32[]{:S(2)}) collective-permute-start(f32[128,128]{1,0:T(8,128)S(1)} %get-tuple-element.42), channel_id=1, source_target_pairs={{0,4},{4,8},{8,12},{12,16},{16,20},{20,24},{24,28},{28,0},{1,5},{5... | collective-permute-start | bytes 196616 | tf_op jit(solution)/shard_map/ppermute | solution.py:12
  11.4 3.1 %collective-permute-start.1 = (f32[128,128]{1,0:T(8,128)S(1)}, f32[128,128]{1,0:T(8,128)S(1)}, u32[]{:S(2)}, u32[]{:S(2)}) collective-permute-start(f32[128,128]{1,0:T(8,128)S(1)} %get-tuple-element.44), channel_id=1, source_target_pairs={{0,28},{4,0},{8,4},{12,8},{16,12},{20,16},{24,20},{28,24},{1,29},{... | collective-permute-start | bytes 196616 | tf_op jit(solution)/shard_map/ppermute | solution.py:12
  14.5 1.7 collective-permute-start.3
  28.8 4.7 %collective-permute-start.5 = (f32[128,128]{1,0:T(8,128)S(1)}, f32[128,128]{1,0:T(8,128)S(1)}, u32[]{:S(2)}, u32[]{:S(2)}) collective-permute-start(f32[128,128]{1,0:T(8,128)S(1)} %get-tuple-element.40), channel_id=1, source_target_pairs={{0,28},{4,0},{8,4},{12,8},{16,12},{20,16},{24,20},{28,24},{1,29},{... | collective-permute-start | bytes 196616 | tf_op jit(solution)/shard_map/ppermute | solution.py:12
  35.7 1.4 collective-permute-done.6
  48.3 1.8 collective-permute-start.10
  50.2 4.7 %collective-permute-start.9 = (f32[128,128]{1,0:T(8,128)S(1)}, f32[128,128]{1,0:T(8,128)S(1)}, u32[]{:S(2)}, u32[]{:S(2)}) collective-permute-start(f32[128,128]{1,0:T(8,128)S(1)} %get-tuple-element.36), channel_id=1, source_target_pairs={{0,28},{4,0},{8,4},{12,8},{16,12},{20,16},{24,20},{28,24},{1,29},{... | collective-permute-start | bytes 196616 | tf_op jit(solution)/shard_map/ppermute | solution.py:12
  55.0 2.3 collective-permute-done.8
  65.7 1.4 convolution_add_fusion.29
  70.0 4.7 %collective-permute-start.13 = (f32[128,128]{1,0:T(8,128)S(1)}, f32[128,128]{1,0:T(8,128)S(1)}, u32[]{:S(2)}, u32[]{:S(2)}) collective-permute-start(f32[128,128]{1,0:T(8,128)S(1)} %get-tuple-element.32), channel_id=1, source_target_pairs={{0,28},{4,0},{8,4},{12,8},{16,12},{20,16},{24,20},{28,24},{1,29},{... | collective-permute-start | bytes 196616 | tf_op jit(solution)/shard_map/ppermute | solution.py:12
  74.7 1.7 collective-permute-start.15
  77.0 1.4 collective-permute-done.14
  78.5 1.6 gather_fusion.25
  88.4 1.4 convolution_add_fusion.24
  93.3 4.7 %collective-permute-start.17 = (f32[128,128]{1,0:T(8,128)}, f32[128,128]{1,0:T(8,128)S(1)}, u32[]{:S(2)}, u32[]{:S(2)}) collective-permute-start(f32[128,128]{1,0:T(8,128)} %get-tuple-element.28), channel_id=1, source_target_pairs={{0,28},{4,0},{8,4},{12,8},{16,12},{20,16},{24,20},{28,24},{1,29},{... | collective-permute-start | bytes 196616 | tf_op jit(solution)/shard_map/ppermute | solution.py:12
  101.7 1.6 gather_fusion.33
  104.4 1.4 gather_fusion.34
  105.8 1.4 gather_fusion.35
  107.1 1.4 gather_fusion.36
  108.5 1.4 gather_fusion.37
  109.9 1.4 gather_fusion.38
  111.3 1.4 gather_fusion.39
  112.7 1.4 fusion.46
  114.1 1.4 convolution_add_fusion.19
  119.7 4.7 %collective-permute-start.21 = (f32[128,128]{1,0:T(8,128)S(1)}, f32[128,128]{1,0:T(8,128)S(1)}, u32[]{:S(2)}, u32[]{:S(2)}) collective-permute-start(f32[128,128]{1,0:T(8,128)S(1)} %get-tuple-element.24), channel_id=1, source_target_pairs={{0,28},{4,0},{8,4},{12,8},{16,12},{20,16},{24,20},{28,24},{1,29},{... | collective-permute-start | bytes 196616 | tf_op jit(solution)/shard_map/ppermute | solution.py:12
  128.9 1.6 gather_fusion.41
  132.3 1.4 gather_fusion.43
  133.7 1.4 gather_fusion.44
  135.0 1.4 gather_fusion.45
  136.4 1.4 gather_fusion.46
  137.8 1.4 gather_fusion.47
  139.6 1.4 convolution_add_fusion.14
  145.2 4.7 %collective-permute-start.25 = (f32[128,128]{1,0:T(8,128)S(1)}, f32[128,128]{1,0:T(8,128)S(1)}, u32[]{:S(2)}, u32[]{:S(2)}) collective-permute-start(f32[128,128]{1,0:T(8,128)S(1)} %get-tuple-element.20), channel_id=1, source_target_pairs={{0,28},{4,0},{8,4},{12,8},{16,12},{20,16},{24,20},{28,24},{1,29},{... | collective-permute-start | bytes 196616 | tf_op jit(solution)/shard_map/ppermute | solution.py:12
  154.4 1.6 gather_fusion.49
  157.8 1.4 gather_fusion.51
  159.2 1.4 gather_fusion.52
  160.5 1.4 gather_fusion.53
  161.9 1.4 gather_fusion.54
  163.3 1.4 gather_fusion.55
  165.1 1.4 convolution_add_fusion.9
  169.6 4.7 %collective-permute-start.29 = (f32[128,128]{1,0:T(8,128)S(1)}, f32[128,128]{1,0:T(8,128)S(1)}, u32[]{:S(2)}, u32[]{:S(2)}) collective-permute-start(f32[128,128]{1,0:T(8,128)S(1)} %get-tuple-element.16), channel_id=1, source_target_pairs={{0,28},{4,0},{8,4},{12,8},{16,12},{20,16},{24,20},{28,24},{1,29},{... | collective-permute-start | bytes 196616 | tf_op jit(solution)/shard_map/ppermute | solution.py:12
  176.5 1.4 collective-permute-done.30
  179.8 1.4 gather_fusion.59
  181.2 1.4 gather_fusion.60
  182.6 1.4 gather_fusion.61
  184.0 1.4 gather_fusion.62
  190.5 38.8 %psum.7 = f32[128]{0:T(128)S(1)} all-reduce(f32[128]{0:T(128)S(1)} %fusion.58), channel_id=1, replica_groups=mesh['patch'=8,'sub'=4] {'patch','sub'}, use_global_device_ids=true, to_apply=%region_2.3 | all-reduce | flops 128 | bytes 1024 | tf_op jit(solution)/shard_map/psum | solution.py:69
  (265 shorter events, 89.6 us)
Async XLA Ops:
  7.2 20.2 %copy-start.2 = (f32[65537]{0:T(1024)}, f32[65537]{0:T(1024)S(1)}, u32[]{:S(2)}) copy-start(f32[65537]{0:T(1024)S(1)} %scatter_custom_fusion) | copy-start | bytes 786448
  7.3 10.4 %copy-start.43 = (s32[1,512]{1,0:T(1,128)S(1)}, s32[1,512]{1,0:T(1,128)}, u32[]{:S(2)}) copy-start(s32[1,512]{1,0:T(1,128)} %param.12) | copy-start | bytes 6148
  7.3 10.4 %copy-start.36 = (s32[4,6]{1,0:T(4,128)S(1)}, s32[4,6]{1,0:T(4,128)}, u32[]{:S(2)}) copy-start(s32[4,6]{1,0:T(4,128)} %param.10) | copy-start | bytes 292
  8.4 9.8 %collective-permute-start = (f32[128,128]{1,0:T(8,128)S(1)}, f32[128,128]{1,0:T(8,128)S(1)}, u32[]{:S(2)}, u32[]{:S(2)}) collective-permute-start(f32[128,128]{1,0:T(8,128)S(1)} %get-tuple-element.42), channel_id=1, source_target_pairs={{0,4},{4,8},{8,12},{12,16},{16,20},{20,24},{24,28},{28,0},{1,5},{5... | collective-permute-start | bytes 196616 | tf_op jit(solution)/shard_map/ppermute | solution.py:12
  11.4 6.7 %collective-permute-start.1 = (f32[128,128]{1,0:T(8,128)S(1)}, f32[128,128]{1,0:T(8,128)S(1)}, u32[]{:S(2)}, u32[]{:S(2)}) collective-permute-start(f32[128,128]{1,0:T(8,128)S(1)} %get-tuple-element.44), channel_id=1, source_target_pairs={{0,28},{4,0},{8,4},{12,8},{16,12},{20,16},{24,20},{28,24},{1,29},{... | collective-permute-start | bytes 196616 | tf_op jit(solution)/shard_map/ppermute | solution.py:12
  14.5 3.7 %collective-permute-start.2 = (f32[128,128]{1,0:T(8,128)S(1)}, f32[128,128]{1,0:T(8,128)S(1)}, u32[]{:S(2)}, u32[]{:S(2)}) collective-permute-start(f32[128,128]{1,0:T(8,128)S(1)} %get-tuple-element.43), channel_id=1, source_target_pairs={{0,1},{1,2},{2,3},{3,0},{4,5},{5,6},{6,7},{7,4},{8,9},{9,10},{10,1... | collective-permute-start | bytes 196616 | tf_op jit(solution)/shard_map/ppermute | solution.py:12
  14.5 3.7 %collective-permute-start.3 = (f32[128,128]{1,0:T(8,128)S(1)}, f32[128,128]{1,0:T(8,128)S(1)}, u32[]{:S(2)}, u32[]{:S(2)}) collective-permute-start(f32[128,128]{1,0:T(8,128)S(1)} %get-tuple-element.45), channel_id=1, source_target_pairs={{0,3},{1,0},{2,1},{3,2},{4,7},{5,4},{6,5},{7,6},{8,11},{9,8},{10,9... | collective-permute-start | bytes 196616 | tf_op jit(solution)/shard_map/ppermute | solution.py:12
  18.0 63.1 %copy-start.38 = (s32[1024]{0:T(1024)}, s32[1024]{0:T(1024)S(1)}, u32[]{:S(2)}) copy-start(s32[1024]{0:T(1024)S(1)} %get-tuple-element.53) | copy-start | bytes 12292
  18.0 63.6 %copy-start.37 = (s32[1024]{0:T(1024)}, s32[1024]{0:T(1024)S(1)}, u32[]{:S(2)}) copy-start(s32[1024]{0:T(1024)S(1)} %get-tuple-element.52) | copy-start | bytes 12292
  18.1 64.9 %copy-start.40 = (s32[1024]{0:T(1024)}, s32[1024]{0:T(1024)S(1)}, u32[]{:S(2)}) copy-start(s32[1024]{0:T(1024)S(1)} %get-tuple-element.51) | copy-start | bytes 12292
  18.1 66.1 %copy-start.39 = (s32[1024]{0:T(1024)}, s32[1024]{0:T(1024)S(1)}, u32[]{:S(2)}) copy-start(s32[1024]{0:T(1024)S(1)} %get-tuple-element.50) | copy-start | bytes 12292
  18.1 67.4 %copy-start.42 = (s32[1024]{0:T(1024)}, s32[1024]{0:T(1024)S(1)}, u32[]{:S(2)}) copy-start(s32[1024]{0:T(1024)S(1)} %get-tuple-element.49) | copy-start | bytes 12292
  18.1 68.6 %copy-start.41 = (s32[1024]{0:T(1024)}, s32[1024]{0:T(1024)S(1)}, u32[]{:S(2)}) copy-start(s32[1024]{0:T(1024)S(1)} %get-tuple-element.48) | copy-start | bytes 12292
  19.3 4.8 %copy-start = (f32[4,6,128,128]{3,2,1,0:T(8,128)S(1)}, f32[4,6,128,128]{3,2,1,0:T(8,128)}, u32[]{:S(2)}) copy-start(f32[4,6,128,128]{3,2,1,0:T(8,128)} %param.9) | copy-start | bytes 4718596
  28.7 7.0 %collective-permute-start.4 = (f32[128,128]{1,0:T(8,128)S(1)}, f32[128,128]{1,0:T(8,128)S(1)}, u32[]{:S(2)}, u32[]{:S(2)}) collective-permute-start(f32[128,128]{1,0:T(8,128)S(1)} %get-tuple-element.38), channel_id=1, source_target_pairs={{0,4},{4,8},{8,12},{12,16},{16,20},{20,24},{24,28},{28,0},{1,5},{5... | collective-permute-start | bytes 196616 | tf_op jit(solution)/shard_map/ppermute | solution.py:12
  28.8 7.0 %collective-permute-start.5 = (f32[128,128]{1,0:T(8,128)S(1)}, f32[128,128]{1,0:T(8,128)S(1)}, u32[]{:S(2)}, u32[]{:S(2)}) collective-permute-start(f32[128,128]{1,0:T(8,128)S(1)} %get-tuple-element.40), channel_id=1, source_target_pairs={{0,28},{4,0},{8,4},{12,8},{16,12},{20,16},{24,20},{28,24},{1,29},{... | collective-permute-start | bytes 196616 | tf_op jit(solution)/shard_map/ppermute | solution.py:12
  33.5 3.7 %collective-permute-start.6 = (f32[128,128]{1,0:T(8,128)S(1)}, f32[128,128]{1,0:T(8,128)S(1)}, u32[]{:S(2)}, u32[]{:S(2)}) collective-permute-start(f32[128,128]{1,0:T(8,128)S(1)} %get-tuple-element.39), channel_id=1, source_target_pairs={{0,1},{1,2},{2,3},{3,0},{4,5},{5,6},{6,7},{7,4},{8,9},{9,10},{10,1... | collective-permute-start | bytes 196616 | tf_op jit(solution)/shard_map/ppermute | solution.py:12
  34.7 2.5 %collective-permute-start.7 = (f32[128,128]{1,0:T(8,128)S(1)}, f32[128,128]{1,0:T(8,128)S(1)}, u32[]{:S(2)}, u32[]{:S(2)}) collective-permute-start(f32[128,128]{1,0:T(8,128)S(1)} %get-tuple-element.41), channel_id=1, source_target_pairs={{0,3},{1,0},{2,1},{3,2},{4,7},{5,4},{6,5},{7,6},{8,11},{9,8},{10,9... | collective-permute-start | bytes 196616 | tf_op jit(solution)/shard_map/ppermute | solution.py:12
  48.3 6.7 %collective-permute-start.10 = (f32[128,128]{1,0:T(8,128)S(1)}, f32[128,128]{1,0:T(8,128)S(1)}, u32[]{:S(2)}, u32[]{:S(2)}) collective-permute-start(f32[128,128]{1,0:T(8,128)S(1)} %get-tuple-element.35), channel_id=1, source_target_pairs={{0,1},{1,2},{2,3},{3,0},{4,5},{5,6},{6,7},{7,4},{8,9},{9,10},{10,1... | collective-permute-start | bytes 196616 | tf_op jit(solution)/shard_map/ppermute | solution.py:12
  50.1 4.9 %collective-permute-start.11 = (f32[128,128]{1,0:T(8,128)S(1)}, f32[128,128]{1,0:T(8,128)S(1)}, u32[]{:S(2)}, u32[]{:S(2)}) collective-permute-start(f32[128,128]{1,0:T(8,128)S(1)} %get-tuple-element.37), channel_id=1, source_target_pairs={{0,3},{1,0},{2,1},{3,2},{4,7},{5,4},{6,5},{7,6},{8,11},{9,8},{10,9... | collective-permute-start | bytes 196616 | tf_op jit(solution)/shard_map/ppermute | solution.py:12
  50.2 7.1 %collective-permute-start.8 = (f32[128,128]{1,0:T(8,128)S(1)}, f32[128,128]{1,0:T(8,128)S(1)}, u32[]{:S(2)}, u32[]{:S(2)}) collective-permute-start(f32[128,128]{1,0:T(8,128)S(1)} %get-tuple-element.34), channel_id=1, source_target_pairs={{0,4},{4,8},{8,12},{12,16},{16,20},{20,24},{24,28},{28,0},{1,5},{5... | collective-permute-start | bytes 196616 | tf_op jit(solution)/shard_map/ppermute | solution.py:12
  50.2 7.1 %collective-permute-start.9 = (f32[128,128]{1,0:T(8,128)S(1)}, f32[128,128]{1,0:T(8,128)S(1)}, u32[]{:S(2)}, u32[]{:S(2)}) collective-permute-start(f32[128,128]{1,0:T(8,128)S(1)} %get-tuple-element.36), channel_id=1, source_target_pairs={{0,28},{4,0},{8,4},{12,8},{16,12},{20,16},{24,20},{28,24},{1,29},{... | collective-permute-start | bytes 196616 | tf_op jit(solution)/shard_map/ppermute | solution.py:12
  70.0 7.0 %collective-permute-start.12 = (f32[128,128]{1,0:T(8,128)S(1)}, f32[128,128]{1,0:T(8,128)S(1)}, u32[]{:S(2)}, u32[]{:S(2)}) collective-permute-start(f32[128,128]{1,0:T(8,128)S(1)} %get-tuple-element.30), channel_id=1, source_target_pairs={{0,4},{4,8},{8,12},{12,16},{16,20},{20,24},{24,28},{28,0},{1,5},{5... | collective-permute-start | bytes 196616 | tf_op jit(solution)/shard_map/ppermute | solution.py:12
  70.0 7.0 %collective-permute-start.13 = (f32[128,128]{1,0:T(8,128)S(1)}, f32[128,128]{1,0:T(8,128)S(1)}, u32[]{:S(2)}, u32[]{:S(2)}) collective-permute-start(f32[128,128]{1,0:T(8,128)S(1)} %get-tuple-element.32), channel_id=1, source_target_pairs={{0,28},{4,0},{8,4},{12,8},{16,12},{20,16},{24,20},{28,24},{1,29},{... | collective-permute-start | bytes 196616 | tf_op jit(solution)/shard_map/ppermute | solution.py:12
  74.7 3.7 %collective-permute-start.14 = (f32[128,128]{1,0:T(8,128)S(1)}, f32[128,128]{1,0:T(8,128)S(1)}, u32[]{:S(2)}, u32[]{:S(2)}) collective-permute-start(f32[128,128]{1,0:T(8,128)S(1)} %get-tuple-element.31), channel_id=1, source_target_pairs={{0,1},{1,2},{2,3},{3,0},{4,5},{5,6},{6,7},{7,4},{8,9},{9,10},{10,1... | collective-permute-start | bytes 196616 | tf_op jit(solution)/shard_map/ppermute | solution.py:12
  74.7 3.7 %collective-permute-start.15 = (f32[128,128]{1,0:T(8,128)S(1)}, f32[128,128]{1,0:T(8,128)S(1)}, u32[]{:S(2)}, u32[]{:S(2)}) collective-permute-start(f32[128,128]{1,0:T(8,128)S(1)} %get-tuple-element.33), channel_id=1, source_target_pairs={{0,3},{1,0},{2,1},{3,2},{4,7},{5,4},{6,5},{7,6},{8,11},{9,8},{10,9... | collective-permute-start | bytes 196616 | tf_op jit(solution)/shard_map/ppermute | solution.py:12
  93.3 7.2 %collective-permute-start.16 = (f32[128,128]{1,0:T(8,128)}, f32[128,128]{1,0:T(8,128)S(1)}, u32[]{:S(2)}, u32[]{:S(2)}) collective-permute-start(f32[128,128]{1,0:T(8,128)} %get-tuple-element.26), channel_id=1, source_target_pairs={{0,4},{4,8},{8,12},{12,16},{16,20},{20,24},{24,28},{28,0},{1,5},{5... | collective-permute-start | bytes 196616 | tf_op jit(solution)/shard_map/ppermute | solution.py:12
  93.3 7.2 %collective-permute-start.17 = (f32[128,128]{1,0:T(8,128)}, f32[128,128]{1,0:T(8,128)S(1)}, u32[]{:S(2)}, u32[]{:S(2)}) collective-permute-start(f32[128,128]{1,0:T(8,128)} %get-tuple-element.28), channel_id=1, source_target_pairs={{0,28},{4,0},{8,4},{12,8},{16,12},{20,16},{24,20},{28,24},{1,29},{... | collective-permute-start | bytes 196616 | tf_op jit(solution)/shard_map/ppermute | solution.py:12
  98.0 3.7 %collective-permute-start.18 = (f32[128,128]{1,0:T(8,128)S(1)}, f32[128,128]{1,0:T(8,128)S(1)}, u32[]{:S(2)}, u32[]{:S(2)}) collective-permute-start(f32[128,128]{1,0:T(8,128)S(1)} %get-tuple-element.27), channel_id=1, source_target_pairs={{0,1},{1,2},{2,3},{3,0},{4,5},{5,6},{6,7},{7,4},{8,9},{9,10},{10,1... | collective-permute-start | bytes 196616 | tf_op jit(solution)/shard_map/ppermute | solution.py:12
  99.1 2.6 %collective-permute-start.19 = (f32[128,128]{1,0:T(8,128)S(1)}, f32[128,128]{1,0:T(8,128)S(1)}, u32[]{:S(2)}, u32[]{:S(2)}) collective-permute-start(f32[128,128]{1,0:T(8,128)S(1)} %get-tuple-element.29), channel_id=1, source_target_pairs={{0,3},{1,0},{2,1},{3,2},{4,7},{5,4},{6,5},{7,6},{8,11},{9,8},{10,9... | collective-permute-start | bytes 196616 | tf_op jit(solution)/shard_map/ppermute | solution.py:12
  112.7 2.8 %copy-start.32 = (f32[4,128,128]{2,1,0:T(8,128)S(1)}, f32[4,128,128]{2,1,0:T(8,128)}, u32[]{:S(2)}) copy-start(f32[4,128,128]{2,1,0:T(8,128)} %gather_fusion.36) | copy-start | bytes 786436
  112.7 3.2 %copy-start.26 = (f32[4,128,128]{2,1,0:T(8,128)S(1)}, f32[4,128,128]{2,1,0:T(8,128)}, u32[]{:S(2)}) copy-start(f32[4,128,128]{2,1,0:T(8,128)} %gather_fusion.37) | copy-start | bytes 786436
  119.7 7.2 %collective-permute-start.20 = (f32[128,128]{1,0:T(8,128)}, f32[128,128]{1,0:T(8,128)S(1)}, u32[]{:S(2)}, u32[]{:S(2)}) collective-permute-start(f32[128,128]{1,0:T(8,128)} %get-tuple-element.22), channel_id=1, source_target_pairs={{0,4},{4,8},{8,12},{12,16},{16,20},{20,24},{24,28},{28,0},{1,5},{5... | collective-permute-start | bytes 196616 | tf_op jit(solution)/shard_map/ppermute | solution.py:12
  119.7 7.2 %collective-permute-start.21 = (f32[128,128]{1,0:T(8,128)S(1)}, f32[128,128]{1,0:T(8,128)S(1)}, u32[]{:S(2)}, u32[]{:S(2)}) collective-permute-start(f32[128,128]{1,0:T(8,128)S(1)} %get-tuple-element.24), channel_id=1, source_target_pairs={{0,28},{4,0},{8,4},{12,8},{16,12},{20,16},{24,20},{28,24},{1,29},{... | collective-permute-start | bytes 196616 | tf_op jit(solution)/shard_map/ppermute | solution.py:12
  124.4 3.7 %collective-permute-start.22 = (f32[128,128]{1,0:T(8,128)S(1)}, f32[128,128]{1,0:T(8,128)S(1)}, u32[]{:S(2)}, u32[]{:S(2)}) collective-permute-start(f32[128,128]{1,0:T(8,128)S(1)} %get-tuple-element.23), channel_id=1, source_target_pairs={{0,1},{1,2},{2,3},{3,0},{4,5},{5,6},{6,7},{7,4},{8,9},{9,10},{10,1... | collective-permute-start | bytes 196616 | tf_op jit(solution)/shard_map/ppermute | solution.py:12
  125.5 2.6 %collective-permute-start.23 = (f32[128,128]{1,0:T(8,128)S(1)}, f32[128,128]{1,0:T(8,128)}, u32[]{:S(2)}, u32[]{:S(2)}) collective-permute-start(f32[128,128]{1,0:T(8,128)S(1)} %get-tuple-element.25), channel_id=1, source_target_pairs={{0,3},{1,0},{2,1},{3,2},{4,7},{5,4},{6,5},{7,6},{8,11},{9,8},{10,9... | collective-permute-start | bytes 196616 | tf_op jit(solution)/shard_map/ppermute | solution.py:12
  145.2 7.2 %collective-permute-start.24 = (f32[128,128]{1,0:T(8,128)}, f32[128,128]{1,0:T(8,128)S(1)}, u32[]{:S(2)}, u32[]{:S(2)}) collective-permute-start(f32[128,128]{1,0:T(8,128)} %get-tuple-element.18), channel_id=1, source_target_pairs={{0,4},{4,8},{8,12},{12,16},{16,20},{20,24},{24,28},{28,0},{1,5},{5... | collective-permute-start | bytes 196616 | tf_op jit(solution)/shard_map/ppermute | solution.py:12
  145.2 7.2 %collective-permute-start.25 = (f32[128,128]{1,0:T(8,128)S(1)}, f32[128,128]{1,0:T(8,128)S(1)}, u32[]{:S(2)}, u32[]{:S(2)}) collective-permute-start(f32[128,128]{1,0:T(8,128)S(1)} %get-tuple-element.20), channel_id=1, source_target_pairs={{0,28},{4,0},{8,4},{12,8},{16,12},{20,16},{24,20},{28,24},{1,29},{... | collective-permute-start | bytes 196616 | tf_op jit(solution)/shard_map/ppermute | solution.py:12
  149.9 3.7 %collective-permute-start.26 = (f32[128,128]{1,0:T(8,128)S(1)}, f32[128,128]{1,0:T(8,128)S(1)}, u32[]{:S(2)}, u32[]{:S(2)}) collective-permute-start(f32[128,128]{1,0:T(8,128)S(1)} %get-tuple-element.19), channel_id=1, source_target_pairs={{0,1},{1,2},{2,3},{3,0},{4,5},{5,6},{6,7},{7,4},{8,9},{9,10},{10,1... | collective-permute-start | bytes 196616 | tf_op jit(solution)/shard_map/ppermute | solution.py:12
  151.1 2.5 %collective-permute-start.27 = (f32[128,128]{1,0:T(8,128)S(1)}, f32[128,128]{1,0:T(8,128)}, u32[]{:S(2)}, u32[]{:S(2)}) collective-permute-start(f32[128,128]{1,0:T(8,128)S(1)} %get-tuple-element.21), channel_id=1, source_target_pairs={{0,3},{1,0},{2,1},{3,2},{4,7},{5,4},{6,5},{7,6},{8,11},{9,8},{10,9... | collective-permute-start | bytes 196616 | tf_op jit(solution)/shard_map/ppermute | solution.py:12
  165.1 2.2 copy-start.21
  168.4 21.9 %copy-start.1 = (f32[512,128]{1,0:T(8,128)}, f32[512,128]{1,0:T(8,128)S(1)}, u32[]{:S(2)}) copy-start(f32[512,128]{1,0:T(8,128)S(1)} %fusion.62) | copy-start | bytes 786436
  169.5 7.0 %collective-permute-start.28 = (f32[128,128]{1,0:T(8,128)S(1)}, f32[128,128]{1,0:T(8,128)S(1)}, u32[]{:S(2)}, u32[]{:S(2)}) collective-permute-start(f32[128,128]{1,0:T(8,128)S(1)} %get-tuple-element.14), channel_id=1, source_target_pairs={{0,4},{4,8},{8,12},{12,16},{16,20},{20,24},{24,28},{28,0},{1,5},{5... | collective-permute-start | bytes 196616 | tf_op jit(solution)/shard_map/ppermute | solution.py:12
  169.6 7.0 %collective-permute-start.29 = (f32[128,128]{1,0:T(8,128)S(1)}, f32[128,128]{1,0:T(8,128)S(1)}, u32[]{:S(2)}, u32[]{:S(2)}) collective-permute-start(f32[128,128]{1,0:T(8,128)S(1)} %get-tuple-element.16), channel_id=1, source_target_pairs={{0,28},{4,0},{8,4},{12,8},{16,12},{20,16},{24,20},{28,24},{1,29},{... | collective-permute-start | bytes 196616 | tf_op jit(solution)/shard_map/ppermute | solution.py:12
  174.3 3.7 %collective-permute-start.30 = (f32[128,128]{1,0:T(8,128)S(1)}, f32[128,128]{1,0:T(8,128)S(1)}, u32[]{:S(2)}, u32[]{:S(2)}) collective-permute-start(f32[128,128]{1,0:T(8,128)S(1)} %get-tuple-element.15), channel_id=1, source_target_pairs={{0,1},{1,2},{2,3},{3,0},{4,5},{5,6},{6,7},{7,4},{8,9},{9,10},{10,1... | collective-permute-start | bytes 196616 | tf_op jit(solution)/shard_map/ppermute | solution.py:12
  175.4 2.5 %collective-permute-start.31 = (f32[128,128]{1,0:T(8,128)S(1)}, f32[128,128]{1,0:T(8,128)S(1)}, u32[]{:S(2)}, u32[]{:S(2)}) collective-permute-start(f32[128,128]{1,0:T(8,128)S(1)} %get-tuple-element.17), channel_id=1, source_target_pairs={{0,3},{1,0},{2,1},{3,2},{4,7},{5,4},{6,5},{7,6},{8,11},{9,8},{10,9... | collective-permute-start | bytes 196616 | tf_op jit(solution)/shard_map/ppermute | solution.py:12
  186.0 3.1 %copy-start.16 = (f32[4,128,128]{2,1,0:T(8,128)S(1)}, f32[4,128,128]{2,1,0:T(8,128)}, u32[]{:S(2)}) copy-start(f32[4,128,128]{2,1,0:T(8,128)} %gather_fusion.61) | copy-start | bytes 786436
  186.4 3.1 %copy-start.15 = (f32[4,128,128]{2,1,0:T(8,128)S(1)}, f32[4,128,128]{2,1,0:T(8,128)}, u32[]{:S(2)}) copy-start(f32[4,128,128]{2,1,0:T(8,128)} %gather_fusion.62) | copy-start | bytes 786436
  (28 other events, 46.2 us)
where the time goes:
time: 231 us; the launch traced here: 230 us
  local copies, waits for them, and re-layouts  78.7 us (34%)
  starting transfers between devices  53.4 us (23%)
  blocking collectives  38.8 us (17%)
  matrix products  28 us (12%)
  waiting for transfers between devices  13.6 us (6%)
  other arithmetic  11.9 us (5%)
  between operations  5.44 us (2%)
    gather x48, local copies, waits for them, and re-layouts, operate(): extended[tile_cols[:, slot_index]]  54.6 us
    ppermute x32, starting transfers between devices, shifted(): return lax.ppermute(value, axis, pairs)  53.4 us
    psum x1, blocking collectives, on_device(): squares = lax.psum(jnp.sum(final * final, axis=0), ('patch', 'sub'))  38.8 us
    dot_general x48, matrix products, operate(): jnp.einsum('bij,bjk->bik', tiles[:, slot_index], extended[tile_cols[:, sl...  28 us
    ppermute x32, waiting for transfers between devices, shifted(): return lax.ppermute(value, axis, pairs)  13.6 us
    gather x8, local copies, waits for them, and re-layouts, operate(): halo_rows = received[receives]  10.7 us
    gather x8, local copies, waits for them, and re-layouts, operate(): packed = field[sends]  8.28 us
  transfers between devices with their start and end apart: 32, of which 13 were waited for; matrix products, arithmetic and copies ran while one was open for 0% of the time, Pallas kernels for 0%

commit v1 on v0

--- a/solution.py
+++ b/solution.py
@@ -66,7 +66,9 @@
             )
             damping = damping_next
     final = right_side - operate(solution)
-    squares = lax.psum(jnp.sum(final * final, axis=0), ("patch", "sub"))
+    squares = jnp.sum(final * final, axis=0)
+    for name in ("sub", "patch"):
+        squares = lax.psum(squares, name)
     return (solution, jnp.sqrt(squares))
 
 

time: 231 us -> 219 us (0.948)
  blocking collectives: 38.8 us -> 26.9 us
    psum x1 -> x2, blocking collectives: 38.8 us -> 26.9 us  [on_device(): squares = lax.psum(squares, name)]
where the time goes in v1:
time: 219 us; the launch traced here: 218 us
  local copies, waits for them, and re-layouts  78.9 us (36%)
  starting transfers between devices  53.4 us (24%)
  matrix products  28 us (13%)
  blocking collectives  26.9 us (12%)
  waiting for transfers between devices  13.6 us (6%)
  other arithmetic  11.9 us (5%)
  between operations  5.44 us (2%)
    gather x48, local copies, waits for them, and re-layouts, operate(): extended[tile_cols[:, slot_index]]  54.8 us
    ppermute x32, starting transfers between devices, shifted(): return lax.ppermute(value, axis, pairs)  53.4 us
    dot_general x48, matrix products, operate(): jnp.einsum('bij,bjk->bik', tiles[:, slot_index], extended[tile_cols[:, sl...  28 us
    psum x2, blocking collectives, on_device(): squares = lax.psum(squares, name)  26.9 us
    ppermute x32, waiting for transfers between devices, shifted(): return lax.ppermute(value, axis, pairs)  13.6 us
    gather x8, local copies, waits for them, and re-layouts, operate(): halo_rows = received[receives]  10.7 us
    gather x8, local copies, waits for them, and re-layouts, operate(): packed = field[sends]  8.28 us
  transfers between devices with their start and end apart: 32, of which 13 were waited for; matrix products, arithmetic and copies ran while one was open for 0% of the time, Pallas kernels for 0%

profile of v1, /device:TPU:0, one launch (start us, length us, event | category | flops | bytes accessed | tf_op | source)
XLA Modules:
  0.0 218.1 jit_solution(14049678176131938214)
XLA Ops:
  4.9 2.3 %scatter_custom_fusion = f32[65537]{0:T(1024)S(1)} fusion(s32[256]{0:T(256)S(1)} %reshape.649, f32[256]{0:T(256)S(1)} %broadcast.65, f32[]{:T(128)} %constant.13.clone.1), kind=kCustom, calls=%fused_computation.254 | custom fusion | flops 256 | bytes 262152 | tf_op jit(solution)/shard_map/scatter-add | solution.py:28
  8.4 3.1 %collective-permute-start = (f32[128,128]{1,0:T(8,128)S(1)}, f32[128,128]{1,0:T(8,128)S(1)}, u32[]{:S(2)}, u32[]{:S(2)}) collective-permute-start(f32[128,128]{1,0:T(8,128)S(1)} %get-tuple-element.42), channel_id=1, source_target_pairs={{0,4},{4,8},{8,12},{12,16},{16,20},{20,24},{24,28},{28,0},{1,5},{5... | collective-permute-start | bytes 196616 | tf_op jit(solution)/shard_map/ppermute | solution.py:12
  11.4 3.1 %collective-permute-start.1 = (f32[128,128]{1,0:T(8,128)S(1)}, f32[128,128]{1,0:T(8,128)S(1)}, u32[]{:S(2)}, u32[]{:S(2)}) collective-permute-start(f32[128,128]{1,0:T(8,128)S(1)} %get-tuple-element.44), channel_id=1, source_target_pairs={{0,28},{4,0},{8,4},{12,8},{16,12},{20,16},{24,20},{28,24},{1,29},{... | collective-permute-start | bytes 196616 | tf_op jit(solution)/shard_map/ppermute | solution.py:12
  14.5 1.7 collective-permute-start.3
  28.8 4.7 %collective-permute-start.5 = (f32[128,128]{1,0:T(8,128)S(1)}, f32[128,128]{1,0:T(8,128)S(1)}, u32[]{:S(2)}, u32[]{:S(2)}) collective-permute-start(f32[128,128]{1,0:T(8,128)S(1)} %get-tuple-element.40), channel_id=1, source_target_pairs={{0,28},{4,0},{8,4},{12,8},{16,12},{20,16},{24,20},{28,24},{1,29},{... | collective-permute-start | bytes 196616 | tf_op jit(solution)/shard_map/ppermute | solution.py:12
  35.7 1.4 collective-permute-done.6
  48.4 1.8 collective-permute-start.10
  50.2 4.7 %collective-permute-start.9 = (f32[128,128]{1,0:T(8,128)S(1)}, f32[128,128]{1,0:T(8,128)S(1)}, u32[]{:S(2)}, u32[]{:S(2)}) collective-permute-start(f32[128,128]{1,0:T(8,128)S(1)} %get-tuple-element.36), channel_id=1, source_target_pairs={{0,28},{4,0},{8,4},{12,8},{16,12},{20,16},{24,20},{28,24},{1,29},{... | collective-permute-start | bytes 196616 | tf_op jit(solution)/shard_map/ppermute | solution.py:12
  55.1 2.3 %collective-permute-done.8 = f32[128,128]{1,0:T(8,128)S(1)} collective-permute-done((f32[128,128]{1,0:T(8,128)S(1)}, f32[128,128]{1,0:T(8,128)S(1)}, u32[]{:S(2)}, u32[]{:S(2)}) %collective-permute-start.8) | collective-permute-done | bytes 65568 | tf_op jit(solution)/shard_map/ppermute | solution.py:12
  65.8 1.4 convolution_add_fusion.29
  70.1 4.7 %collective-permute-start.13 = (f32[128,128]{1,0:T(8,128)S(1)}, f32[128,128]{1,0:T(8,128)S(1)}, u32[]{:S(2)}, u32[]{:S(2)}) collective-permute-start(f32[128,128]{1,0:T(8,128)S(1)} %get-tuple-element.32), channel_id=1, source_target_pairs={{0,28},{4,0},{8,4},{12,8},{16,12},{20,16},{24,20},{28,24},{1,29},{... | collective-permute-start | bytes 196616 | tf_op jit(solution)/shard_map/ppermute | solution.py:12
  74.8 1.7 collective-permute-start.15
  77.0 1.4 collective-permute-done.14
  78.5 1.6 gather_fusion.25
  88.5 1.4 convolution_add_fusion.24
  93.4 4.7 %collective-permute-start.17 = (f32[128,128]{1,0:T(8,128)}, f32[128,128]{1,0:T(8,128)S(1)}, u32[]{:S(2)}, u32[]{:S(2)}) collective-permute-start(f32[128,128]{1,0:T(8,128)} %get-tuple-element.28), channel_id=1, source_target_pairs={{0,28},{4,0},{8,4},{12,8},{16,12},{20,16},{24,20},{28,24},{1,29},{... | collective-permute-start | bytes 196616 | tf_op jit(solution)/shard_map/ppermute | solution.py:12
  101.8 1.6 gather_fusion.33
  104.5 1.4 gather_fusion.34
  105.8 1.4 gather_fusion.35
  107.2 1.4 gather_fusion.36
  108.6 1.4 gather_fusion.37
  110.0 1.4 gather_fusion.38
  111.4 1.4 gather_fusion.39
  112.8 1.4 fusion.46
  119.7 4.7 %collective-permute-start.21 = (f32[128,128]{1,0:T(8,128)S(1)}, f32[128,128]{1,0:T(8,128)S(1)}, u32[]{:S(2)}, u32[]{:S(2)}) collective-permute-start(f32[128,128]{1,0:T(8,128)S(1)} %get-tuple-element.24), channel_id=1, source_target_pairs={{0,28},{4,0},{8,4},{12,8},{16,12},{20,16},{24,20},{28,24},{1,29},{... | collective-permute-start | bytes 196616 | tf_op jit(solution)/shard_map/ppermute | solution.py:12
  129.0 1.6 gather_fusion.41
  132.3 1.4 gather_fusion.43
  133.8 1.4 gather_fusion.44
  135.1 1.4 gather_fusion.45
  136.5 1.4 gather_fusion.46
  137.9 1.4 gather_fusion.47
  139.7 1.4 convolution_add_fusion.14
  145.3 4.7 %collective-permute-start.25 = (f32[128,128]{1,0:T(8,128)S(1)}, f32[128,128]{1,0:T(8,128)S(1)}, u32[]{:S(2)}, u32[]{:S(2)}) collective-permute-start(f32[128,128]{1,0:T(8,128)S(1)} %get-tuple-element.20), channel_id=1, source_target_pairs={{0,28},{4,0},{8,4},{12,8},{16,12},{20,16},{24,20},{28,24},{1,29},{... | collective-permute-start | bytes 196616 | tf_op jit(solution)/shard_map/ppermute | solution.py:12
  154.6 1.6 gather_fusion.49
  157.9 1.4 gather_fusion.51
  159.3 1.4 gather_fusion.52
  160.7 1.4 gather_fusion.53
  162.1 1.4 gather_fusion.54
  163.5 1.4 gather_fusion.55
  165.3 1.4 convolution_add_fusion.9
  169.7 4.7 %collective-permute-start.29 = (f32[128,128]{1,0:T(8,128)S(1)}, f32[128,128]{1,0:T(8,128)S(1)}, u32[]{:S(2)}, u32[]{:S(2)}) collective-permute-start(f32[128,128]{1,0:T(8,128)S(1)} %get-tuple-element.16), channel_id=1, source_target_pairs={{0,28},{4,0},{8,4},{12,8},{16,12},{20,16},{24,20},{28,24},{1,29},{... | collective-permute-start | bytes 196616 | tf_op jit(solution)/shard_map/ppermute | solution.py:12
  176.6 1.4 collective-permute-done.30
  179.9 1.4 gather_fusion.59
  181.3 1.4 gather_fusion.60
  182.7 1.4 gather_fusion.61
  184.1 1.4 gather_fusion.62
  190.7 7.4 %psum.14 = f32[128]{0:T(128)S(1)} all-reduce(f32[128]{0:T(128)S(1)} %fusion.58), channel_id=1, replica_groups=mesh['patch'=8,'sub'=4] {'sub'}, use_global_device_ids=true, to_apply=%region_2.3 | all-reduce | flops 128 | bytes 1024 | tf_op jit(solution)/shard_map/psum | solution.py:71
  198.1 19.5 %psum.15 = f32[128]{0:T(128)S(1)} all-reduce(f32[128]{0:T(128)S(1)} %psum.14), channel_id=1, replica_groups=mesh['patch'=8,'sub'=4] {'patch'}, use_global_device_ids=true, to_apply=%region_3.4 | all-reduce | flops 128 | bytes 1024 | tf_op jit(solution)/shard_map/psum | solution.py:71
  (266 shorter events, 91.0 us)
Async XLA Ops:
  7.2 20.3 %copy-start.2 = (f32[65537]{0:T(1024)}, f32[65537]{0:T(1024)S(1)}, u32[]{:S(2)}) copy-start(f32[65537]{0:T(1024)S(1)} %scatter_custom_fusion) | copy-start | bytes 786448
  7.3 10.4 %copy-start.43 = (s32[1,512]{1,0:T(1,128)S(1)}, s32[1,512]{1,0:T(1,128)}, u32[]{:S(2)}) copy-start(s32[1,512]{1,0:T(1,128)} %param.12) | copy-start | bytes 6148
  7.3 10.4 %copy-start.36 = (s32[4,6]{1,0:T(4,128)S(1)}, s32[4,6]{1,0:T(4,128)}, u32[]{:S(2)}) copy-start(s32[4,6]{1,0:T(4,128)} %param.10) | copy-start | bytes 292
  8.4 9.8 %collective-permute-start = (f32[128,128]{1,0:T(8,128)S(1)}, f32[128,128]{1,0:T(8,128)S(1)}, u32[]{:S(2)}, u32[]{:S(2)}) collective-permute-start(f32[128,128]{1,0:T(8,128)S(1)} %get-tuple-element.42), channel_id=1, source_target_pairs={{0,4},{4,8},{8,12},{12,16},{16,20},{20,24},{24,28},{28,0},{1,5},{5... | collective-permute-start | bytes 196616 | tf_op jit(solution)/shard_map/ppermute | solution.py:12
  11.4 6.7 %collective-permute-start.1 = (f32[128,128]{1,0:T(8,128)S(1)}, f32[128,128]{1,0:T(8,128)S(1)}, u32[]{:S(2)}, u32[]{:S(2)}) collective-permute-start(f32[128,128]{1,0:T(8,128)S(1)} %get-tuple-element.44), channel_id=1, source_target_pairs={{0,28},{4,0},{8,4},{12,8},{16,12},{20,16},{24,20},{28,24},{1,29},{... | collective-permute-start | bytes 196616 | tf_op jit(solution)/shard_map/ppermute | solution.py:12
  14.5 3.7 %collective-permute-start.2 = (f32[128,128]{1,0:T(8,128)S(1)}, f32[128,128]{1,0:T(8,128)S(1)}, u32[]{:S(2)}, u32[]{:S(2)}) collective-permute-start(f32[128,128]{1,0:T(8,128)S(1)} %get-tuple-element.43), channel_id=1, source_target_pairs={{0,1},{1,2},{2,3},{3,0},{4,5},{5,6},{6,7},{7,4},{8,9},{9,10},{10,1... | collective-permute-start | bytes 196616 | tf_op jit(solution)/shard_map/ppermute | solution.py:12
  14.5 3.7 %collective-permute-start.3 = (f32[128,128]{1,0:T(8,128)S(1)}, f32[128,128]{1,0:T(8,128)S(1)}, u32[]{:S(2)}, u32[]{:S(2)}) collective-permute-start(f32[128,128]{1,0:T(8,128)S(1)} %get-tuple-element.45), channel_id=1, source_target_pairs={{0,3},{1,0},{2,1},{3,2},{4,7},{5,4},{6,5},{7,6},{8,11},{9,8},{10,9... | collective-permute-start | bytes 196616 | tf_op jit(solution)/shard_map/ppermute | solution.py:12
  18.0 63.1 %copy-start.38 = (s32[1024]{0:T(1024)}, s32[1024]{0:T(1024)S(1)}, u32[]{:S(2)}) copy-start(s32[1024]{0:T(1024)S(1)} %get-tuple-element.53) | copy-start | bytes 12292
  18.0 63.7 %copy-start.37 = (s32[1024]{0:T(1024)}, s32[1024]{0:T(1024)S(1)}, u32[]{:S(2)}) copy-start(s32[1024]{0:T(1024)S(1)} %get-tuple-element.52) | copy-start | bytes 12292
  18.1 64.9 %copy-start.40 = (s32[1024]{0:T(1024)}, s32[1024]{0:T(1024)S(1)}, u32[]{:S(2)}) copy-start(s32[1024]{0:T(1024)S(1)} %get-tuple-element.51) | copy-start | bytes 12292
  18.1 66.2 %copy-start.39 = (s32[1024]{0:T(1024)}, s32[1024]{0:T(1024)S(1)}, u32[]{:S(2)}) copy-start(s32[1024]{0:T(1024)S(1)} %get-tuple-element.50) | copy-start | bytes 12292
  18.1 67.5 %copy-start.42 = (s32[1024]{0:T(1024)}, s32[1024]{0:T(1024)S(1)}, u32[]{:S(2)}) copy-start(s32[1024]{0:T(1024)S(1)} %get-tuple-element.49) | copy-start | bytes 12292
  18.1 68.7 %copy-start.41 = (s32[1024]{0:T(1024)}, s32[1024]{0:T(1024)S(1)}, u32[]{:S(2)}) copy-start(s32[1024]{0:T(1024)S(1)} %get-tuple-element.48) | copy-start | bytes 12292
  19.3 4.9 %copy-start = (f32[4,6,128,128]{3,2,1,0:T(8,128)S(1)}, f32[4,6,128,128]{3,2,1,0:T(8,128)}, u32[]{:S(2)}) copy-start(f32[4,6,128,128]{3,2,1,0:T(8,128)} %param.9) | copy-start | bytes 4718596
  28.7 7.0 %collective-permute-start.4 = (f32[128,128]{1,0:T(8,128)S(1)}, f32[128,128]{1,0:T(8,128)S(1)}, u32[]{:S(2)}, u32[]{:S(2)}) collective-permute-start(f32[128,128]{1,0:T(8,128)S(1)} %get-tuple-element.38), channel_id=1, source_target_pairs={{0,4},{4,8},{8,12},{12,16},{16,20},{20,24},{24,28},{28,0},{1,5},{5... | collective-permute-start | bytes 196616 | tf_op jit(solution)/shard_map/ppermute | solution.py:12
  28.8 7.0 %collective-permute-start.5 = (f32[128,128]{1,0:T(8,128)S(1)}, f32[128,128]{1,0:T(8,128)S(1)}, u32[]{:S(2)}, u32[]{:S(2)}) collective-permute-start(f32[128,128]{1,0:T(8,128)S(1)} %get-tuple-element.40), channel_id=1, source_target_pairs={{0,28},{4,0},{8,4},{12,8},{16,12},{20,16},{24,20},{28,24},{1,29},{... | collective-permute-start | bytes 196616 | tf_op jit(solution)/shard_map/ppermute | solution.py:12
  33.5 3.7 %collective-permute-start.6 = (f32[128,128]{1,0:T(8,128)S(1)}, f32[128,128]{1,0:T(8,128)S(1)}, u32[]{:S(2)}, u32[]{:S(2)}) collective-permute-start(f32[128,128]{1,0:T(8,128)S(1)} %get-tuple-element.39), channel_id=1, source_target_pairs={{0,1},{1,2},{2,3},{3,0},{4,5},{5,6},{6,7},{7,4},{8,9},{9,10},{10,1... | collective-permute-start | bytes 196616 | tf_op jit(solution)/shard_map/ppermute | solution.py:12
  34.7 2.5 %collective-permute-start.7 = (f32[128,128]{1,0:T(8,128)S(1)}, f32[128,128]{1,0:T(8,128)S(1)}, u32[]{:S(2)}, u32[]{:S(2)}) collective-permute-start(f32[128,128]{1,0:T(8,128)S(1)} %get-tuple-element.41), channel_id=1, source_target_pairs={{0,3},{1,0},{2,1},{3,2},{4,7},{5,4},{6,5},{7,6},{8,11},{9,8},{10,9... | collective-permute-start | bytes 196616 | tf_op jit(solution)/shard_map/ppermute | solution.py:12
  48.4 6.7 %collective-permute-start.10 = (f32[128,128]{1,0:T(8,128)S(1)}, f32[128,128]{1,0:T(8,128)S(1)}, u32[]{:S(2)}, u32[]{:S(2)}) collective-permute-start(f32[128,128]{1,0:T(8,128)S(1)} %get-tuple-element.35), channel_id=1, source_target_pairs={{0,1},{1,2},{2,3},{3,0},{4,5},{5,6},{6,7},{7,4},{8,9},{9,10},{10,1... | collective-permute-start | bytes 196616 | tf_op jit(solution)/shard_map/ppermute | solution.py:12
  50.1 4.9 %collective-permute-start.11 = (f32[128,128]{1,0:T(8,128)S(1)}, f32[128,128]{1,0:T(8,128)S(1)}, u32[]{:S(2)}, u32[]{:S(2)}) collective-permute-start(f32[128,128]{1,0:T(8,128)S(1)} %get-tuple-element.37), channel_id=1, source_target_pairs={{0,3},{1,0},{2,1},{3,2},{4,7},{5,4},{6,5},{7,6},{8,11},{9,8},{10,9... | collective-permute-start | bytes 196616 | tf_op jit(solution)/shard_map/ppermute | solution.py:12
  50.2 7.1 %collective-permute-start.8 = (f32[128,128]{1,0:T(8,128)S(1)}, f32[128,128]{1,0:T(8,128)S(1)}, u32[]{:S(2)}, u32[]{:S(2)}) collective-permute-start(f32[128,128]{1,0:T(8,128)S(1)} %get-tuple-element.34), channel_id=1, source_target_pairs={{0,4},{4,8},{8,12},{12,16},{16,20},{20,24},{24,28},{28,0},{1,5},{5... | collective-permute-start | bytes 196616 | tf_op jit(solution)/shard_map/ppermute | solution.py:12
  50.2 7.1 %collective-permute-start.9 = (f32[128,128]{1,0:T(8,128)S(1)}, f32[128,128]{1,0:T(8,128)S(1)}, u32[]{:S(2)}, u32[]{:S(2)}) collective-permute-start(f32[128,128]{1,0:T(8,128)S(1)} %get-tuple-element.36), channel_id=1, source_target_pairs={{0,28},{4,0},{8,4},{12,8},{16,12},{20,16},{24,20},{28,24},{1,29},{... | collective-permute-start | bytes 196616 | tf_op jit(solution)/shard_map/ppermute | solution.py:12
  70.0 7.0 %collective-permute-start.12 = (f32[128,128]{1,0:T(8,128)S(1)}, f32[128,128]{1,0:T(8,128)S(1)}, u32[]{:S(2)}, u32[]{:S(2)}) collective-permute-start(f32[128,128]{1,0:T(8,128)S(1)} %get-tuple-element.30), channel_id=1, source_target_pairs={{0,4},{4,8},{8,12},{12,16},{16,20},{20,24},{24,28},{28,0},{1,5},{5... | collective-permute-start | bytes 196616 | tf_op jit(solution)/shard_map/ppermute | solution.py:12
  70.1 7.0 %collective-permute-start.13 = (f32[128,128]{1,0:T(8,128)S(1)}, f32[128,128]{1,0:T(8,128)S(1)}, u32[]{:S(2)}, u32[]{:S(2)}) collective-permute-start(f32[128,128]{1,0:T(8,128)S(1)} %get-tuple-element.32), channel_id=1, source_target_pairs={{0,28},{4,0},{8,4},{12,8},{16,12},{20,16},{24,20},{28,24},{1,29},{... | collective-permute-start | bytes 196616 | tf_op jit(solution)/shard_map/ppermute | solution.py:12
  74.8 3.7 %collective-permute-start.14 = (f32[128,128]{1,0:T(8,128)S(1)}, f32[128,128]{1,0:T(8,128)S(1)}, u32[]{:S(2)}, u32[]{:S(2)}) collective-permute-start(f32[128,128]{1,0:T(8,128)S(1)} %get-tuple-element.31), channel_id=1, source_target_pairs={{0,1},{1,2},{2,3},{3,0},{4,5},{5,6},{6,7},{7,4},{8,9},{9,10},{10,1... | collective-permute-start | bytes 196616 | tf_op jit(solution)/shard_map/ppermute | solution.py:12
  74.8 3.7 %collective-permute-start.15 = (f32[128,128]{1,0:T(8,128)S(1)}, f32[128,128]{1,0:T(8,128)S(1)}, u32[]{:S(2)}, u32[]{:S(2)}) collective-permute-start(f32[128,128]{1,0:T(8,128)S(1)} %get-tuple-element.33), channel_id=1, source_target_pairs={{0,3},{1,0},{2,1},{3,2},{4,7},{5,4},{6,5},{7,6},{8,11},{9,8},{10,9... | collective-permute-start | bytes 196616 | tf_op jit(solution)/shard_map/ppermute | solution.py:12
  93.4 7.2 %collective-permute-start.16 = (f32[128,128]{1,0:T(8,128)}, f32[128,128]{1,0:T(8,128)S(1)}, u32[]{:S(2)}, u32[]{:S(2)}) collective-permute-start(f32[128,128]{1,0:T(8,128)} %get-tuple-element.26), channel_id=1, source_target_pairs={{0,4},{4,8},{8,12},{12,16},{16,20},{20,24},{24,28},{28,0},{1,5},{5... | collective-permute-start | bytes 196616 | tf_op jit(solution)/shard_map/ppermute | solution.py:12
  93.4 7.2 %collective-permute-start.17 = (f32[128,128]{1,0:T(8,128)}, f32[128,128]{1,0:T(8,128)S(1)}, u32[]{:S(2)}, u32[]{:S(2)}) collective-permute-start(f32[128,128]{1,0:T(8,128)} %get-tuple-element.28), channel_id=1, source_target_pairs={{0,28},{4,0},{8,4},{12,8},{16,12},{20,16},{24,20},{28,24},{1,29},{... | collective-permute-start | bytes 196616 | tf_op jit(solution)/shard_map/ppermute | solution.py:12
  98.1 3.7 %collective-permute-start.18 = (f32[128,128]{1,0:T(8,128)S(1)}, f32[128,128]{1,0:T(8,128)S(1)}, u32[]{:S(2)}, u32[]{:S(2)}) collective-permute-start(f32[128,128]{1,0:T(8,128)S(1)} %get-tuple-element.27), channel_id=1, source_target_pairs={{0,1},{1,2},{2,3},{3,0},{4,5},{5,6},{6,7},{7,4},{8,9},{9,10},{10,1... | collective-permute-start | bytes 196616 | tf_op jit(solution)/shard_map/ppermute | solution.py:12
  99.2 2.6 %collective-permute-start.19 = (f32[128,128]{1,0:T(8,128)S(1)}, f32[128,128]{1,0:T(8,128)S(1)}, u32[]{:S(2)}, u32[]{:S(2)}) collective-permute-start(f32[128,128]{1,0:T(8,128)S(1)} %get-tuple-element.29), channel_id=1, source_target_pairs={{0,3},{1,0},{2,1},{3,2},{4,7},{5,4},{6,5},{7,6},{8,11},{9,8},{10,9... | collective-permute-start | bytes 196616 | tf_op jit(solution)/shard_map/ppermute | solution.py:12
  112.8 2.8 %copy-start.32 = (f32[4,128,128]{2,1,0:T(8,128)S(1)}, f32[4,128,128]{2,1,0:T(8,128)}, u32[]{:S(2)}) copy-start(f32[4,128,128]{2,1,0:T(8,128)} %gather_fusion.36) | copy-start | bytes 786436
  112.8 3.2 %copy-start.26 = (f32[4,128,128]{2,1,0:T(8,128)S(1)}, f32[4,128,128]{2,1,0:T(8,128)}, u32[]{:S(2)}) copy-start(f32[4,128,128]{2,1,0:T(8,128)} %gather_fusion.37) | copy-start | bytes 786436
  119.7 7.2 %collective-permute-start.20 = (f32[128,128]{1,0:T(8,128)}, f32[128,128]{1,0:T(8,128)S(1)}, u32[]{:S(2)}, u32[]{:S(2)}) collective-permute-start(f32[128,128]{1,0:T(8,128)} %get-tuple-element.22), channel_id=1, source_target_pairs={{0,4},{4,8},{8,12},{12,16},{16,20},{20,24},{24,28},{28,0},{1,5},{5... | collective-permute-start | bytes 196616 | tf_op jit(solution)/shard_map/ppermute | solution.py:12
  119.7 7.2 %collective-permute-start.21 = (f32[128,128]{1,0:T(8,128)S(1)}, f32[128,128]{1,0:T(8,128)S(1)}, u32[]{:S(2)}, u32[]{:S(2)}) collective-permute-start(f32[128,128]{1,0:T(8,128)S(1)} %get-tuple-element.24), channel_id=1, source_target_pairs={{0,28},{4,0},{8,4},{12,8},{16,12},{20,16},{24,20},{28,24},{1,29},{... | collective-permute-start | bytes 196616 | tf_op jit(solution)/shard_map/ppermute | solution.py:12
  124.5 3.7 %collective-permute-start.22 = (f32[128,128]{1,0:T(8,128)S(1)}, f32[128,128]{1,0:T(8,128)S(1)}, u32[]{:S(2)}, u32[]{:S(2)}) collective-permute-start(f32[128,128]{1,0:T(8,128)S(1)} %get-tuple-element.23), channel_id=1, source_target_pairs={{0,1},{1,2},{2,3},{3,0},{4,5},{5,6},{6,7},{7,4},{8,9},{9,10},{10,1... | collective-permute-start | bytes 196616 | tf_op jit(solution)/shard_map/ppermute | solution.py:12
  125.5 2.6 %collective-permute-start.23 = (f32[128,128]{1,0:T(8,128)S(1)}, f32[128,128]{1,0:T(8,128)}, u32[]{:S(2)}, u32[]{:S(2)}) collective-permute-start(f32[128,128]{1,0:T(8,128)S(1)} %get-tuple-element.25), channel_id=1, source_target_pairs={{0,3},{1,0},{2,1},{3,2},{4,7},{5,4},{6,5},{7,6},{8,11},{9,8},{10,9... | collective-permute-start | bytes 196616 | tf_op jit(solution)/shard_map/ppermute | solution.py:12
  145.3 7.2 %collective-permute-start.24 = (f32[128,128]{1,0:T(8,128)}, f32[128,128]{1,0:T(8,128)S(1)}, u32[]{:S(2)}, u32[]{:S(2)}) collective-permute-start(f32[128,128]{1,0:T(8,128)} %get-tuple-element.18), channel_id=1, source_target_pairs={{0,4},{4,8},{8,12},{12,16},{16,20},{20,24},{24,28},{28,0},{1,5},{5... | collective-permute-start | bytes 196616 | tf_op jit(solution)/shard_map/ppermute | solution.py:12
  145.3 7.2 %collective-permute-start.25 = (f32[128,128]{1,0:T(8,128)S(1)}, f32[128,128]{1,0:T(8,128)S(1)}, u32[]{:S(2)}, u32[]{:S(2)}) collective-permute-start(f32[128,128]{1,0:T(8,128)S(1)} %get-tuple-element.20), channel_id=1, source_target_pairs={{0,28},{4,0},{8,4},{12,8},{16,12},{20,16},{24,20},{28,24},{1,29},{... | collective-permute-start | bytes 196616 | tf_op jit(solution)/shard_map/ppermute | solution.py:12
  150.0 3.7 %collective-permute-start.26 = (f32[128,128]{1,0:T(8,128)S(1)}, f32[128,128]{1,0:T(8,128)S(1)}, u32[]{:S(2)}, u32[]{:S(2)}) collective-permute-start(f32[128,128]{1,0:T(8,128)S(1)} %get-tuple-element.19), channel_id=1, source_target_pairs={{0,1},{1,2},{2,3},{3,0},{4,5},{5,6},{6,7},{7,4},{8,9},{9,10},{10,1... | collective-permute-start | bytes 196616 | tf_op jit(solution)/shard_map/ppermute | solution.py:12
  151.2 2.5 %collective-permute-start.27 = (f32[128,128]{1,0:T(8,128)S(1)}, f32[128,128]{1,0:T(8,128)}, u32[]{:S(2)}, u32[]{:S(2)}) collective-permute-start(f32[128,128]{1,0:T(8,128)S(1)} %get-tuple-element.21), channel_id=1, source_target_pairs={{0,3},{1,0},{2,1},{3,2},{4,7},{5,4},{6,5},{7,6},{8,11},{9,8},{10,9... | collective-permute-start | bytes 196616 | tf_op jit(solution)/shard_map/ppermute | solution.py:12
  165.2 2.2 %copy-start.21 = (f32[4,128,128]{2,1,0:T(8,128)S(1)}, f32[4,128,128]{2,1,0:T(8,128)}, u32[]{:S(2)}) copy-start(f32[4,128,128]{2,1,0:T(8,128)} %gather_fusion.54) | copy-start | bytes 786436
  168.5 22.0 %copy-start.1 = (f32[512,128]{1,0:T(8,128)}, f32[512,128]{1,0:T(8,128)S(1)}, u32[]{:S(2)}) copy-start(f32[512,128]{1,0:T(8,128)S(1)} %fusion.62) | copy-start | bytes 786436
  169.6 7.0 %collective-permute-start.28 = (f32[128,128]{1,0:T(8,128)S(1)}, f32[128,128]{1,0:T(8,128)S(1)}, u32[]{:S(2)}, u32[]{:S(2)}) collective-permute-start(f32[128,128]{1,0:T(8,128)S(1)} %get-tuple-element.14), channel_id=1, source_target_pairs={{0,4},{4,8},{8,12},{12,16},{16,20},{20,24},{24,28},{28,0},{1,5},{5... | collective-permute-start | bytes 196616 | tf_op jit(solution)/shard_map/ppermute | solution.py:12
  169.7 7.0 %collective-permute-start.29 = (f32[128,128]{1,0:T(8,128)S(1)}, f32[128,128]{1,0:T(8,128)S(1)}, u32[]{:S(2)}, u32[]{:S(2)}) collective-permute-start(f32[128,128]{1,0:T(8,128)S(1)} %get-tuple-element.16), channel_id=1, source_target_pairs={{0,28},{4,0},{8,4},{12,8},{16,12},{20,16},{24,20},{28,24},{1,29},{... | collective-permute-start | bytes 196616 | tf_op jit(solution)/shard_map/ppermute | solution.py:12
  174.4 3.7 %collective-permute-start.30 = (f32[128,128]{1,0:T(8,128)S(1)}, f32[128,128]{1,0:T(8,128)S(1)}, u32[]{:S(2)}, u32[]{:S(2)}) collective-permute-start(f32[128,128]{1,0:T(8,128)S(1)} %get-tuple-element.15), channel_id=1, source_target_pairs={{0,1},{1,2},{2,3},{3,0},{4,5},{5,6},{6,7},{7,4},{8,9},{9,10},{10,1... | collective-permute-start | bytes 196616 | tf_op jit(solution)/shard_map/ppermute | solution.py:12
  175.6 2.5 %collective-permute-start.31 = (f32[128,128]{1,0:T(8,128)S(1)}, f32[128,128]{1,0:T(8,128)S(1)}, u32[]{:S(2)}, u32[]{:S(2)}) collective-permute-start(f32[128,128]{1,0:T(8,128)S(1)} %get-tuple-element.17), channel_id=1, source_target_pairs={{0,3},{1,0},{2,1},{3,2},{4,7},{5,4},{6,5},{7,6},{8,11},{9,8},{10,9... | collective-permute-start | bytes 196616 | tf_op jit(solution)/shard_map/ppermute | solution.py:12
  186.2 3.1 %copy-start.16 = (f32[4,128,128]{2,1,0:T(8,128)S(1)}, f32[4,128,128]{2,1,0:T(8,128)}, u32[]{:S(2)}) copy-start(f32[4,128,128]{2,1,0:T(8,128)} %gather_fusion.61) | copy-start | bytes 786436
  186.6 3.1 %copy-start.15 = (f32[4,128,128]{2,1,0:T(8,128)S(1)}, f32[4,128,128]{2,1,0:T(8,128)}, u32[]{:S(2)}) copy-start(f32[4,128,128]{2,1,0:T(8,128)} %gather_fusion.62) | copy-start | bytes 786436
  (28 other events, 46.3 us)
